TPU v7x, 32 devices: a whole 2x2x4 slice. The times are simulated.
32 devices in a mesh: owner: 4 (over y, core), rows: 8 (over z, x).
Axes of the slice: x: 2, y: 2, z: 4, core: 2. Of those that a mesh axis runs over, the one named last changes fastest.
Arguments:
- train_gate: float32 [64, 2048, 1024], P('owner', 'rows'), may hold values from -0.1875 to 0.1875
- other_gate: bfloat16 [64, 2048, 1024], P('owner', 'rows'), may hold values from -0.0625 to 0.0625
- train_up: float32 [64, 2048, 1024], P('owner', 'rows'), may hold values from -0.1875 to 0.1875
- other_up: bfloat16 [64, 2048, 1024], P('owner', 'rows'), may hold values from -0.0625 to 0.0625
- train_down: float32 [64, 1024, 2048], P('owner', None, 'rows'), may hold values from -0.25 to 0.25
- other_down: bfloat16 [64, 1024, 2048], P('owner', None, 'rows'), may hold values from -0.09375 to 0.09375
- router_weight: float32 [2048, 64], P('rows', 'owner'), may hold values from -0.125 to 0.125
- router_gain: float32 [2048], P('rows'), may hold values from 0.25 to 1.75
Outputs:
- ready_gate: bfloat16 [64, 2048, 1024], P('owner', None, 'rows')
- ready_up: bfloat16 [64, 2048, 1024], P('owner', None, 'rows')
- ready_down: bfloat16 [64, 1024, 2048], P('owner', 'rows')
- scale_gate: float32 [64, 1024], P('owner', 'rows')
- scale_up: float32 [64, 1024], P('owner', 'rows')
- scale_down: float32 [64, 1024], P('owner', 'rows')
- serve_router: bfloat16 [2048, 64], replicated
All inputs are finite; a program needn't handle non-finite values. Where the computation divides by a largest or mean magnitude, that divisor is 1e-20 or more.
Results may differ from a plain program's by a relative error of at most 0.001.
Values may be sent and summed in bfloat16 or wider, within the bound.
A program may use at most 192 MiB of HBM per device.

v0:
```python
import jax
import jax.numpy as jnp
from jax import lax
from jax.sharding import PartitionSpec as P


def shards(
    train_gate, other_gate, train_up, other_up, train_down, other_down, router_weight, router_gain
):
    latest_gate = train_gate + other_gate.astype(jnp.float32)
    latest_up = train_up + other_up.astype(jnp.float32)
    latest_down = train_down + other_down.astype(jnp.float32)
    scale_gate, scale_up, scale_down = lax.pmax(
        (
            jnp.max(jnp.abs(latest_gate), axis=1),
            jnp.max(jnp.abs(latest_up), axis=1),
            jnp.max(jnp.abs(latest_down), axis=2),
        ),
        "rows",
    )
    narrow_gate, narrow_up, narrow_down = (
        (latest_gate / jnp.expand_dims(scale_gate, 1)).astype(jnp.bfloat16),
        (latest_up / jnp.expand_dims(scale_up, 1)).astype(jnp.bfloat16),
        (latest_down / jnp.expand_dims(scale_down, 2)).astype(jnp.bfloat16),
    )
    ready_gate, ready_up = (
        lax.all_to_all(narrow_gate, "rows", split_axis=2, concat_axis=1, tiled=True),
        lax.all_to_all(narrow_up, "rows", split_axis=2, concat_axis=1, tiled=True),
    )
    ready_down = lax.all_to_all(narrow_down, "rows", split_axis=1, concat_axis=2, tiled=True)
    scale_gate = lax.dynamic_slice_in_dim(
        scale_gate, lax.axis_index("rows") * ready_gate.shape[2], ready_gate.shape[2], axis=1
    )
    scale_up = lax.dynamic_slice_in_dim(
        scale_up, lax.axis_index("rows") * ready_up.shape[2], ready_up.shape[2], axis=1
    )
    scale_down = lax.dynamic_slice_in_dim(
        scale_down, lax.axis_index("rows") * ready_down.shape[1], ready_down.shape[1], axis=1
    )
    part_router = (router_weight * router_gain[:, None]).astype(jnp.bfloat16)
    row_router = lax.all_gather(part_router, "rows", axis=0, tiled=True)
    serve_router = lax.all_gather(row_router, "owner", axis=1, tiled=True)
    return (ready_gate, ready_up, ready_down, scale_gate, scale_up, scale_down, serve_router)


def solution(mesh):
    placed = (
        P("owner", "rows", None),
        P("owner", "rows", None),
        P("owner", "rows", None),
        P("owner", "rows", None),
        P("owner", None, "rows"),
        P("owner", None, "rows"),
        P("rows", "owner"),
        P("rows"),
    )
    return jax.shard_map(
        shards,
        mesh=mesh,
        in_specs=placed,
        out_specs=(
            P("owner", None, "rows"),
            P("owner", None, "rows"),
            P("owner", "rows", None),
            P("owner", "rows"),
            P("owner", "rows"),
            P("owner", "rows"),
            P(),
        ),
        check_vma=False,
    )
```

profile of v0, /device:TPU:0, one launch (start us, length us, event | category | flops | bytes accessed | tf_op | source)
XLA Modules:
  0.0 877.2 jit_solution(6322543164802641597)
XLA Ops:
  7.2 0.0 all-reduce.3.cloned.1.call-start
  7.2 17.6 %copy.34 = f32[16,256,1024]{1,0,2:T(8,128)} copy(f32[16,256,1024]{2,1,0:T(8,128)} %param.10) | data formatting | bytes 33554432 | tf_op args[2]
  24.8 12.5 %copy.33 = bf16[16,256,1024]{1,0,2:T(8,128)(2,1)} copy(bf16[16,256,1024]{2,1,0:T(8,128)(2,1)} %param.11) | data formatting | bytes 16777216 | tf_op args[3]
  37.3 17.6 %copy.31 = f32[16,256,1024]{1,0,2:T(8,128)} copy(f32[16,256,1024]{2,1,0:T(8,128)} %param.8) | data formatting | bytes 33554432 | tf_op args[0]
  54.9 12.5 %copy.30 = bf16[16,256,1024]{1,0,2:T(8,128)(2,1)} copy(bf16[16,256,1024]{2,1,0:T(8,128)(2,1)} %param.9) | data formatting | bytes 16777216 | tf_op args[1]
  67.4 11.1 %abs_reduce_fusion.1 = f32[16,1024]{0,1:T(8,128)} fusion(f32[16,256,1024]{1,0,2:T(8,128)} %copy.34, bf16[16,256,1024]{1,0,2:T(8,128)(2,1)} %copy.33), kind=kLoop, calls=%fused_computation.4 | loop fusion | flops 16760832 | bytes 25231360 | tf_op jit(solution)/shard_map/reduce_max | solution.py:16
  78.5 2.1 copy-done
  80.6 2.4 copy-done.1
  83.0 4.3 abs_reduce_fusion.2
  87.3 0.0 slice-done
  87.3 29.3 %abs_reduce_fusion = f32[16,1024]{0,1:T(8,128)} fusion(f32[16,1024,256]{2,1,0:T(8,128)} %param.12, bf16[16,1024,256]{2,1,0:T(8,128)(2,1)S(1)} %bitcast.14), kind=kLoop, calls=%fused_computation.2 | loop fusion | flops 16760832 | bytes 25231360 | tf_op jit(solution)/shard_map/reduce_max | solution.py:17
  116.5 0.0 all-reduce.3.cloned.1.call-update
  116.6 92.5 %all-reduce.3.cloned.1.call-done = (f32[16,1024]{0,1:T(8,128)}, f32[16,1024]{0,1:T(8,128)}, f32[16,1024]{0,1:T(8,128)}) async-done(((f32[16,1024]{0,1:T(8,128)}, f32[16,1024]{0,1:T(8,128)}, f32[16,1024]{0,1:T(8,128)}), (f32[16,1024]{0,1:T(8,128)}, f32[16,1024]{0,1:T(8,128)}, f32[16,1024]{0,1:T(8,128)})) %all-reduce.3.cloned.1.call-update) | async-done | bytes 196624 | tf_op jit(solution)/shard_map/pmax | solution.py:13
  209.0 20.5 %divide_convert_fusion.1 = (bf16[16,256,1024]{1,0,2:T(8,128)(2,1)}, bf16[16,256,1024]{1,0,2:T(8,128)(2,1)S(1)}) fusion(f32[16,256,1024]{1,0,2:T(8,128)} %copy.34, bf16[16,256,1024]{1,0,2:T(8,128)(2,1)} %copy.33, f32[16,1024]{0,1:T(8,128)} %get-tuple-element.15, f32[16,1024]{0,1:T(8,128)} %get-tuple-element.14, f32[16,256,1024]{1,0,2:T(8,128)} %copy.31, ...), kind=kLoop, calls=%fused_computation.3 | loop fusion | flops 33554432 | bytes 67239936 | tf_op jit(solution)/shard_map/convert_element_type | solution.py:23
  229.6 187.0 %all_to_all.54 = bf16[16,256,1024]{1,0,2:T(8,128)(2,1)} all-to-all(bf16[16,256,1024]{1,0,2:T(8,128)(2,1)S(1)} %get-tuple-element.18), channel_id=1, replica_groups=mesh['owner'=4,'rows'=8] {'rows'}, dimensions={2} | all-to-all | bytes 16777216 | tf_op jit(solution)/shard_map/all_to_all | solution.py:27
  416.6 4.9 all-to-all-start.1
  421.5 23.8 %divide_convert_fusion = bf16[16,1024,256]{2,0,1:T(8,128)(2,1)} fusion(f32[16,1024,256]{2,1,0:T(8,128)} %param.12, f32[16,1024]{0,1:T(8,128)S(1)} %copy-done.2, bf16[16,1024,256]{2,1,0:T(8,128)(2,1)} %param.13), kind=kLoop, calls=%fused_computation.1 | loop fusion | flops 16777216 | bytes 33619968 | tf_op jit(solution)/shard_map/convert_element_type | solution.py:24
  445.3 158.3 %all-to-all-done.1 = bf16[16,256,1024]{1,0,2:T(8,128)(2,1)} async-done(((bf16[16,256,1024]{1,0,2:T(8,128)(2,1)}), bf16[16,256,1024]{1,0,2:T(8,128)(2,1)}, u32[]{:S(2)}, u32[]{:S(2)}) %all-to-all-start.1) | async-done | bytes 8388640 | tf_op jit(solution)/shard_map/all_to_all | solution.py:28
  603.6 5.0 all-to-all-start.2
  608.7 201.9 %all_gather.6 = bf16[2048,16]{0,1:T(8,128)(2,1)S(1)} all-gather(bf16[256,16]{0,1:T(8,128)(2,1)S(1)} %multiply_convert_fusion), channel_id=1, replica_groups=mesh['owner'=4,'rows'=8] {'rows'}, dimensions={0}, use_global_device_ids=true | all-gather | bytes 73728 | tf_op jit(solution)/shard_map/all_gather | solution.py:41
  810.6 6.0 all_gather.7
  816.5 0.8 constant_dynamic-slice_fusion
  817.4 0.7 copy.40
  818.1 0.7 copy.41
  818.7 0.8 constant_dynamic-slice_fusion.2
  819.6 0.7 copy.39
  820.2 12.3 %copy.32 = bf16[16,8,256,128]{3,2,1,0:T(8,128)(2,1)} copy(bf16[16,8,256,128]{2,0,3,1:T(8,128)(2,1)} %bitcast.15) | data formatting | bytes 16777216 | tf_op jit(solution)/shard_map/all_to_all | solution.py:27
  832.5 12.3 %copy.35 = bf16[16,8,256,128]{3,2,1,0:T(8,128)(2,1)} copy(bf16[16,8,256,128]{2,0,3,1:T(8,128)(2,1)} %bitcast.4) | data formatting | bytes 16777216 | tf_op jit(solution)/shard_map/all_to_all | solution.py:28
  844.8 0.0 all-to-all-done.2
  844.8 11.4 %copy.38 = bf16[16,128,8,256]{3,2,1,0:T(8,128)(2,1)} copy(bf16[16,128,8,256]{3,0,1,2:T(8,128)(2,1)} %bitcast.7) | data formatting | bytes 16777216 | tf_op jit(solution)/shard_map/all_to_all | solution.py:30
  856.2 13.4 %all_to_all.50 = bf16[16,128,2048]{2,1,0:T(8,128)(2,1)} reshape(bf16[16,128,8,256]{3,2,1,0:T(8,128)(2,1)} %copy.38) | data formatting | bytes 16777216 | tf_op jit(solution)/shard_map/all_to_all | solution.py:30
  869.6 0.7 copy.53
  (13 shorter events, 0.0 us)
Async XLA Ops:
  7.2 201.9 %all-reduce.3.cloned.1.call-start = ((), (), s32[]{:S(2)}) async-start(), calls=%async_computation.3 | async-start | bytes 3145728 | tf_op jit(solution)/shard_map/pmax | solution.py:13
  67.4 13.2 %copy-start = (f32[16,256,1024]{1,0,2:T(8,128)S(1)}, f32[16,256,1024]{1,0,2:T(8,128)}, u32[]{:S(2)}) copy-start(f32[16,256,1024]{1,0,2:T(8,128)} %copy.31) | copy-start | bytes 50331652
  67.4 15.6 %copy-start.1 = (bf16[16,256,1024]{1,0,2:T(8,128)(2,1)S(1)}, bf16[16,256,1024]{1,0,2:T(8,128)(2,1)}, u32[]{:S(2)}) copy-start(bf16[16,256,1024]{1,0,2:T(8,128)(2,1)} %copy.30) | copy-start | bytes 25165828
  67.4 19.9 %slice-start = ((s8[8388608]{0:T(1024)(128)(4,1)}), s8[4194304]{0:T(1024)(128)(4,1)S(1)}, s32[]{:S(2)}) async-start(s8[8388608]{0:T(1024)(128)(4,1)} %bitcast.13), calls=%async_computation.4 | async-start | bytes 8388608
  83.0 4.3 slice-start.1
  229.6 192.0 %copy-start.2 = (f32[16,1024]{0,1:T(8,128)S(1)}, f32[16,1024]{0,1:T(8,128)}, u32[]{:S(2)}) copy-start(f32[16,1024]{0,1:T(8,128)} %get-tuple-element.16) | copy-start | bytes 196612
  416.6 187.0 %all-to-all-start.1 = ((bf16[16,256,1024]{1,0,2:T(8,128)(2,1)}), bf16[16,256,1024]{1,0,2:T(8,128)(2,1)}, u32[]{:S(2)}, u32[]{:S(2)}) async-start(bf16[16,256,1024]{1,0,2:T(8,128)(2,1)} %get-tuple-element.17), calls=%async_computation.1 | async-start | bytes 16777216 | tf_op jit(solution)/shard_map/all_to_all | solution.py:28
  445.3 163.3 %copy-start.3 = (f32[256,16]{0,1:T(8,128)S(1)}, f32[256,16]{0,1:T(8,128)}, u32[]{:S(2)}) copy-start(f32[256,16]{0,1:T(8,128)} %param.14) | copy-start | bytes 49156
  445.3 163.3 %copy-start.4 = (f32[256]{0:T(256)S(1)}, f32[256]{0:T(256)}, u32[]{:S(2)}) copy-start(f32[256]{0:T(256)} %param.15) | copy-start | bytes 3076
  603.6 241.2 %all-to-all-start.2 = ((bf16[16,1024,256]{2,0,1:T(8,128)(2,1)}), bf16[16,1024,256]{2,0,1:T(8,128)(2,1)}, u32[]{:S(2)}, u32[]{:S(2)}) async-start(bf16[16,1024,256]{2,0,1:T(8,128)(2,1)} %divide_convert_fusion), calls=%async_computation.2 | async-start | bytes 16777216 | tf_op jit(solution)/shard_map/all_to_all | solution.py:30
Sparse Core Ops, SparseCore 0:
  116.7 92.2 all-reduce.2
where the time goes:
time: 880 us; the launch traced here: 877 us
  blocking collectives  395 us (45%)
  waiting for transfers between devices  251 us (29%)
  local copies, waits for them, and re-layouts  118 us (13%)
  other arithmetic  88.9 us (10%)
  between operations  14.1 us (2%)
  starting transfers between devices  10 us (1%)
    all_gather x1, blocking collectives, shards(): row_router = lax.all_gather(part_router, 'rows', axis=0, tiled=True)  202 us
    all_to_all x1, blocking collectives, shards(): lax.all_to_all(narrow_gate, 'rows', split_axis=2, concat_axis=1, tiled=True)  187 us
    all_to_all x1, waiting for transfers between devices, shards(): lax.all_to_all(narrow_up, 'rows', split_axis=2, concat_axis=1, tiled=True)  158 us
    pmax x1, waiting for transfers between devices, shards(): lax.pmax((jnp.max(jnp.abs(latest_gate), axis=1), jnp.max(jnp.abs(latest_u...  92.5 us
    unnamed x22, local copies, waits for them, and re-layouts  67.4 us
    reduce_max x1, other arithmetic, shards(): jnp.max(jnp.abs(latest_down), axis=2)  29.3 us
    all_to_all x2, local copies, waits for them, and re-layouts, shards(): lax.all_to_all(narrow_down, 'rows', split_axis=1, concat_axis=2, tiled=True)  24.8 us
    convert_element_type x1, other arithmetic, shards(): (latest_down / jnp.expand_dims(scale_down, 2)).astype(jnp.bfloat16)  23.8 us
  transfers between devices with their start and end apart: 3, of which 2 were waited for; matrix products, arithmetic and copies ran while one was open for 6% of the time, Pallas kernels for 0%

commit v1 on v0

--- a/solution.py
+++ b/solution.py
@@ -24,7 +24,12 @@
         (latest_down / jnp.expand_dims(scale_down, 2)).astype(jnp.bfloat16),
     )
     ready_gate, ready_up = (
-        lax.all_to_all(narrow_gate, "rows", split_axis=2, concat_axis=1, tiled=True),
+        jnp.concatenate(
+            lax.all_to_all(
+                jnp.stack(jnp.split(narrow_gate, lax.axis_size("rows"), axis=2)), "rows", 0, 0
+            ),
+            axis=1,
+        ),
         lax.all_to_all(narrow_up, "rows", split_axis=2, concat_axis=1, tiled=True),
     )
     ready_down = lax.all_to_all(narrow_down, "rows", split_axis=1, concat_axis=2, tiled=True)

time: 880 us -> 822 us (0.934)
  blocking collectives: 395 us -> 208 us
  waiting for transfers between devices: 251 us -> 404 us
  local copies, waits for them, and re-layouts: 118 us -> 88.9 us
    all_to_all x1 -> x0, blocking collectives: 187 us -> none  [shards(): lax.all_to_all(narrow_gate, 'rows', split_axis=2, concat_axis=1, tiled=True)]
    all_to_all x1, waiting for transfers between devices: 0.01 us -> 163 us  [shards(): lax.all_to_all(narrow_down, 'rows', split_axis=1, concat_axis=2, tiled=True)]
    unnamed x22 -> x34, local copies, waits for them, and re-layouts: 67.4 us -> 41.2 us
    all_to_all x1 -> x0, local copies, waits for them, and re-layouts: 12.3 us -> none  [shards(): lax.all_to_all(narrow_gate, 'rows', split_axis=2, concat_axis=1, tiled=True)]
    pmax x1, waiting for transfers between devices: 92.5 us -> 82.4 us  [shards(): lax.pmax((jnp.max(jnp.abs(latest_gate), axis=1), jnp.max(jnp.abs(latest_u...]
    convert_element_type x0 -> x1, other arithmetic: none -> 9.39 us  [shards(): (latest_gate / jnp.expand_dims(scale_gate, 1)).astype(jnp.bfloat16)]
  transfers between devices with their start and end apart: 3 -> 4, of which waited for: 2 -> 3; matrix products, arithmetic and copies ran while one was open for 6% -> 8% of each run, Pallas kernels for 0% -> 0%
where the time goes in v1:
time: 822 us; the launch traced here: 820 us
  waiting for transfers between devices  404 us (49%)
  blocking collectives  208 us (25%)
  other arithmetic  89.9 us (11%)
  local copies, waits for them, and re-layouts  88.9 us (11%)
  starting transfers between devices  15.2 us (2%)
  between operations  14.2 us (2%)
    all_gather x1, blocking collectives, shards(): row_router = lax.all_gather(part_router, 'rows', axis=0, tiled=True)  202 us
    all_to_all x1, waiting for transfers between devices, shards(): lax.all_to_all(narrow_down, 'rows', split_axis=1, concat_axis=2, tiled=True)  163 us
    all_to_all x1, waiting for transfers between devices, shards(): lax.all_to_all(narrow_up, 'rows', split_axis=2, concat_axis=1, tiled=True)  159 us
    pmax x1, waiting for transfers between devices, shards(): lax.pmax((jnp.max(jnp.abs(latest_gate), axis=1), jnp.max(jnp.abs(latest_u...  82.4 us
    unnamed x34, local copies, waits for them, and re-layouts  41.2 us
    reduce_max x1, other arithmetic, shards(): jnp.max(jnp.abs(latest_down), axis=2)  30.1 us
    all_to_all x2, local copies, waits for them, and re-layouts, shards(): lax.all_to_all(narrow_down, 'rows', split_axis=1, concat_axis=2, tiled=True)  24.8 us
    convert_element_type x1, other arithmetic, shards(): (latest_down / jnp.expand_dims(scale_down, 2)).astype(jnp.bfloat16)  23.8 us
  transfers between devices with their start and end apart: 4, of which 3 were waited for; matrix products, arithmetic and copies ran while one was open for 8% of the time, Pallas kernels for 0%

profile of v1, /device:TPU:0, one launch (start us, length us, event | category | flops | bytes accessed | tf_op | source)
XLA Modules:
  0.0 820.1 jit_solution(4641286640537155644)
XLA Ops:
  7.2 12.5 %copy.28 = bf16[16,256,1024]{1,0,2:T(8,128)(2,1)} copy(bf16[16,256,1024]{2,1,0:T(8,128)(2,1)} %param.11) | data formatting | bytes 16777216 | tf_op args[3]
  19.7 17.6 %copy.29 = f32[16,256,1024]{1,0,2:T(8,128)} copy(f32[16,256,1024]{2,1,0:T(8,128)} %param.10) | data formatting | bytes 33554432 | tf_op args[2]
  37.3 10.3 %abs_reduce_fusion.2 = f32[16,1024]{1,0:T(8,128)} fusion(f32[16,256,1024]{2,1,0:T(8,128)} %param.8, bf16[16,256,1024]{2,1,0:T(8,128)(2,1)} %param.9), kind=kLoop, calls=%fused_computation.7 | loop fusion | flops 16760832 | bytes 25231360 | tf_op jit(solution)/shard_map/reduce_max | solution.py:15
  47.9 30.1 %abs_reduce_fusion = f32[16,1024]{0,1:T(8,128)} fusion(f32[16,1024,256]{2,1,0:T(8,128)} %param.12, bf16[16,1024,256]{2,1,0:T(8,128)(2,1)S(1)} %copy-done), kind=kLoop, calls=%fused_computation.2 | loop fusion | flops 16760832 | bytes 25231360 | tf_op jit(solution)/shard_map/reduce_max | solution.py:17
  78.1 4.3 abs_reduce_fusion.1
  82.4 82.4 %all-reduce.3.cloned.1.call-done = (f32[16,1024]{1,0:T(8,128)}, f32[16,1024]{0,1:T(8,128)}, f32[16,1024]{0,1:T(8,128)}) async-done(((f32[16,1024]{1,0:T(8,128)}, f32[16,1024]{0,1:T(8,128)}, f32[16,1024]{0,1:T(8,128)}), (f32[16,1024]{1,0:T(8,128)}, f32[16,1024]{0,1:T(8,128)}, f32[16,1024]{0,1:T(8,128)})) %all-reduce.3.cloned.1.call-update) | async-done | bytes 196624 | tf_op jit(solution)/shard_map/pmax | solution.py:13
  164.8 12.1 %divide_convert_fusion.1 = bf16[16,256,1024]{1,0,2:T(8,128)(2,1)} fusion(f32[16,256,1024]{1,0,2:T(8,128)} %copy.29, bf16[16,256,1024]{1,0,2:T(8,128)(2,1)} %copy.28, f32[16,1024]{0,1:T(8,128)} %get-tuple-element.15), kind=kLoop, calls=%fused_computation.3 | loop fusion | flops 16777216 | bytes 33619968 | tf_op jit(solution)/shard_map/convert_element_type | solution.py:23
  176.9 5.3 all-to-all-start.1
  182.1 23.8 %divide_convert_fusion = bf16[16,1024,256]{2,0,1:T(8,128)(2,1)} fusion(f32[16,1024,256]{2,1,0:T(8,128)} %param.12, f32[16,1024]{0,1:T(8,128)S(1)} %copy-done.1, bf16[16,1024,256]{2,1,0:T(8,128)(2,1)} %param.13), kind=kLoop, calls=%fused_computation.1 | loop fusion | flops 16777216 | bytes 33619968 | tf_op jit(solution)/shard_map/convert_element_type | solution.py:24
  205.9 158.7 %all-to-all-done.1 = bf16[16,256,1024]{1,0,2:T(8,128)(2,1)} async-done(((bf16[16,256,1024]{1,0,2:T(8,128)(2,1)}), bf16[16,256,1024]{1,0,2:T(8,128)(2,1)}, u32[]{:S(2)}, u32[]{:S(2)}) %all-to-all-start.1) | async-done | bytes 8388640 | tf_op jit(solution)/shard_map/all_to_all | solution.py:33
  364.7 5.0 all-to-all-start.2
  369.7 9.4 %divide_convert_fusion.2 = bf16[16,256,1024]{2,1,0:T(8,128)(2,1)S(1)} fusion(f32[16,256,1024]{2,1,0:T(8,128)} %param.8, bf16[16,256,1024]{2,1,0:T(8,128)(2,1)} %param.9, f32[16,1024]{1,0:T(8,128)S(1)} %copy-done.2), kind=kLoop, calls=%fused_computation.6 | loop fusion | flops 16777216 | bytes 33619968 | tf_op jit(solution)/shard_map/convert_element_type | solution.py:22
  379.1 1.2 fusion.7
  380.3 1.2 fusion.6
  381.6 1.2 fusion.5
  382.8 1.2 fusion.4
  384.0 1.2 fusion.3
  385.3 1.2 fusion.2
  386.5 1.2 fusion.1
  387.8 1.2 fusion
  389.0 162.5 %all-to-all-done.2 = bf16[16,1024,256]{2,0,1:T(8,128)(2,1)} async-done(((bf16[16,1024,256]{2,0,1:T(8,128)(2,1)}), bf16[16,1024,256]{2,0,1:T(8,128)(2,1)}, u32[]{:S(2)}, u32[]{:S(2)}) %all-to-all-start.2) | async-done | bytes 8388640 | tf_op jit(solution)/shard_map/all_to_all | solution.py:35
  551.6 5.0 all-to-all-start
  556.6 202.2 %all_gather.6 = bf16[2048,16]{0,1:T(8,128)(2,1)S(1)} all-gather(bf16[256,16]{0,1:T(8,128)(2,1)S(1)} %multiply_convert_fusion), channel_id=1, replica_groups=mesh['owner'=4,'rows'=8] {'rows'}, dimensions={0}, use_global_device_ids=true | all-gather | bytes 73728 | tf_op jit(solution)/shard_map/all_gather | solution.py:46
  758.8 6.0 all_gather.7
  764.8 0.8 constant_dynamic-slice_fusion
  765.6 0.7 copy.35
  766.3 0.7 copy.34
  767.6 12.3 %copy.30 = bf16[16,8,256,128]{3,2,1,0:T(8,128)(2,1)} copy(bf16[16,8,256,128]{2,0,3,1:T(8,128)(2,1)} %bitcast.11) | data formatting | bytes 16777216 | tf_op jit(solution)/shard_map/all_to_all | solution.py:33
  779.9 11.4 %copy.33 = bf16[16,128,8,256]{3,2,1,0:T(8,128)(2,1)} copy(bf16[16,128,8,256]{3,0,1,2:T(8,128)(2,1)} %bitcast.14) | data formatting | bytes 16777216 | tf_op jit(solution)/shard_map/all_to_all | solution.py:35
  791.3 13.4 %all_to_all.37 = bf16[16,128,2048]{2,1,0:T(8,128)(2,1)} reshape(bf16[16,128,8,256]{3,2,1,0:T(8,128)(2,1)} %copy.33) | data formatting | bytes 16777216 | tf_op jit(solution)/shard_map/all_to_all | solution.py:35
  804.7 7.9 copy.27
  812.6 0.7 copy.54
  (29 shorter events, 1.0 us)
Async XLA Ops:
  7.2 157.6 %all-reduce.3.cloned.1.call-start = ((), (), s32[]{:S(2)}) async-start(), calls=%async_computation.3 | async-start | bytes 2228224 | tf_op jit(solution)/shard_map/pmax | solution.py:13
  37.3 10.6 %copy-start = (bf16[16,1024,256]{2,1,0:T(8,128)(2,1)S(1)}, bf16[16,1024,256]{2,1,0:T(8,128)(2,1)}, u32[]{:S(2)}) copy-start(bf16[16,1024,256]{2,1,0:T(8,128)(2,1)} %param.13) | copy-start | bytes 25165828
  37.3 40.8 %slice-start = ((s8[16777216]{0:T(1024)(128)(4,1)}), s8[4194304]{0:T(1024)(128)(4,1)S(1)}, s32[]{:S(2)}) async-start(s8[16777216]{0:T(1024)(128)(4,1)} %bitcast.43), calls=%async_computation.4 | async-start | bytes 8388608
  37.3 40.8 %slice-start.1 = ((s8[16777216]{0:T(1024)(128)(4,1)}), s8[4194304]{0:T(1024)(128)(4,1)S(1)}, s32[]{:S(2)}) async-start(s8[16777216]{0:T(1024)(128)(4,1)} %bitcast.43), calls=%async_computation.5 | async-start | bytes 8388608
  37.3 40.8 %slice-start.4 = ((s8[8388608]{0:T(1024)(128)(4,1)}), s8[4194304]{0:T(1024)(128)(4,1)S(1)}, s32[]{:S(2)}) async-start(s8[8388608]{0:T(1024)(128)(4,1)} %bitcast.45), calls=%async_computation.8 | async-start | bytes 8388608
  47.9 30.1 %slice-start.2 = ((s8[16777216]{0:T(1024)(128)(4,1)}), s8[4194304]{0:T(1024)(128)(4,1)S(1)}, s32[]{:S(2)}) async-start(s8[16777216]{0:T(1024)(128)(4,1)} %bitcast.43), calls=%async_computation.6 | async-start | bytes 8388608
  47.9 30.2 %slice-start.3 = ((s8[16777216]{0:T(1024)(128)(4,1)}), s8[4194304]{0:T(1024)(128)(4,1)S(1)}, s32[]{:S(2)}) async-start(s8[16777216]{0:T(1024)(128)(4,1)} %bitcast.43), calls=%async_computation.7 | async-start | bytes 8388608
  47.9 30.2 %slice-start.5 = ((s8[8388608]{0:T(1024)(128)(4,1)}), s8[4194304]{0:T(1024)(128)(4,1)S(1)}, s32[]{:S(2)}) async-start(s8[8388608]{0:T(1024)(128)(4,1)} %bitcast.45), calls=%async_computation.9 | async-start | bytes 8388608
  176.9 5.3 copy-start.1
  176.9 187.8 %all-to-all-start.1 = ((bf16[16,256,1024]{1,0,2:T(8,128)(2,1)}), bf16[16,256,1024]{1,0,2:T(8,128)(2,1)}, u32[]{:S(2)}, u32[]{:S(2)}) async-start(bf16[16,256,1024]{1,0,2:T(8,128)(2,1)} %divide_convert_fusion.1), calls=%async_computation.1 | async-start | bytes 16777216 | tf_op jit(solution)/shard_map/all_to_all | solution.py:33
  205.9 163.7 %copy-start.2 = (f32[16,1024]{1,0:T(8,128)S(1)}, f32[16,1024]{1,0:T(8,128)}, u32[]{:S(2)}) copy-start(f32[16,1024]{1,0:T(8,128)} %get-tuple-element.14) | copy-start | bytes 196612
  364.7 186.9 %all-to-all-start.2 = ((bf16[16,1024,256]{2,0,1:T(8,128)(2,1)}), bf16[16,1024,256]{2,0,1:T(8,128)(2,1)}, u32[]{:S(2)}, u32[]{:S(2)}) async-start(bf16[16,1024,256]{2,0,1:T(8,128)(2,1)} %divide_convert_fusion), calls=%async_computation.2 | async-start | bytes 16777216 | tf_op jit(solution)/shard_map/all_to_all | solution.py:35
  389.0 167.5 %copy-start.3 = (f32[256,16]{0,1:T(8,128)S(1)}, f32[256,16]{0,1:T(8,128)}, u32[]{:S(2)}) copy-start(f32[256,16]{0,1:T(8,128)} %param.14) | copy-start | bytes 49156
  389.0 167.5 %copy-start.4 = (f32[256]{0:T(256)S(1)}, f32[256]{0:T(256)}, u32[]{:S(2)}) copy-start(f32[256]{0:T(256)} %param.15) | copy-start | bytes 3076
  551.6 253.1 %all-to-all-start = ((bf16[8,16,256,128]{3,2,1,0:T(8,128)(2,1)}), bf16[8,16,256,128]{3,2,1,0:T(8,128)(2,1)}, u32[]{:S(2)}, u32[]{:S(2)}) async-start(bf16[8,16,256,128]{3,2,1,0:T(8,128)(2,1)} %fusion), calls=%async_computation | async-start | bytes 16777216 | tf_op jit(solution)/shard_map/all_to_all | solution.py:28
Sparse Core Ops, SparseCore 0:
  82.5 82.2 all-reduce.2
